TPU v7x, 512 devices: a whole 4x8x8 slice. The times are simulated.
512 devices in a mesh: graph: 32 (over z, x), dp: 16 (over y, core).
Axes of the slice: x: 4, y: 8, z: 8, core: 2. Of those that a mesh axis runs over, the one named last changes fastest.
Arguments:
- node_state: bfloat16 [16, 16384, 512], P('dp', 'graph'), may hold values from -6 to 6
- edge_state: bfloat16 [16, 65536, 512], P('dp', 'graph'), may hold values from -6 to 6
- senders: int32 [16, 65536], P('dp', 'graph'), may hold values from 0 to 767
- receivers: int32 [16, 65536], P('dp', 'graph'), may hold values from 0 to 511
- send_index: int32 [16, 32, 256], P('dp', 'graph'), may hold values from 0 to 511
- cotangent: bfloat16 [16, 16384, 512], P('dp', 'graph'), may hold values from -0.046875 to 0.046875
- w_edge: bfloat16 [1536, 512], replicated, may hold values from -0.15625 to 0.15625
- w_node: bfloat16 [1024, 512], replicated, may hold values from -0.1875 to 0.1875
- error_memory: float32 [16, 1024, 512], P('dp', 'graph'), may hold values from -6 to 6
- warm_q: float32 [512, 64], replicated, may hold values from -6 to 6
Outputs:
- new_nodes: bfloat16 [16, 16384, 512], P('dp', 'graph')
- update: float32 [1024, 512], P('graph')
- new_error: float32 [16, 1024, 512], P('dp', 'graph')
- new_q: float32 [512, 64], replicated
All inputs are finite; a program needn't handle non-finite values.
Results may differ from a plain program's by a relative error of at most 0.0066.
Values may be sent and summed in bfloat16 or wider, within the bound.
A program may use at most 64 MiB of HBM per device.

v0:
```python
import jax
import jax.numpy as jnp
from jax import lax
from jax.sharding import Mesh
from jax.sharding import PartitionSpec as P

GRAPH = ("graph_0", "graph_1")
DP = ("dp_0", "dp_1")


def cut_along(shard, dim, count):
    before, after = (shard.shape[:dim], shard.shape[dim + 1 :])
    return jnp.moveaxis(shard.reshape(*before, count, -1, *after), dim, 0)


def summed_on_arrival(shard, axis, dim):
    count = lax.axis_size(axis)
    pieces = lax.all_to_all(cut_along(shard, dim, count), axis, 0, 0, tiled=True)
    return jnp.sum(pieces.astype(jnp.float32), axis=0)


def from_everyone(shard, axis):
    count = lax.axis_size(axis)
    return lax.all_to_all(
        jnp.broadcast_to(shard[None], (count, *shard.shape)), axis, 0, 0, tiled=True
    )


def over_copies(shard, axis):
    return from_everyone(shard, axis).sum(axis=0)


def padded_to(lines, count):
    spare = -lines.shape[0] % count
    if not spare:
        return lines
    return jnp.concatenate([lines, jnp.zeros((spare, *lines.shape[1:]), lines.dtype)])


def in_order(pieces, dim):
    lengths = list(pieces.shape[1:])
    lengths[dim] *= pieces.shape[0]
    return jnp.moveaxis(pieces, 0, dim).reshape(lengths)


def gather_axes(shard, axes, dim):
    far, near = axes
    first = from_everyone(shard, far)
    pieces = jnp.swapaxes(from_everyone(first, near), 0, 1)
    return in_order(pieces.reshape(-1, *shard.shape), dim)


def sum_at_owner(shard, axis, dim):
    pieces = cut_along(shard, dim, lax.axis_size(axis))
    arrived = lax.all_to_all(pieces, axis, split_axis=0, concat_axis=0, tiled=True)
    return arrived.sum(axis=0)


def summed_rows(shard, axes, dim):
    far, near = axes
    own = sum_at_owner(cut_along(shard, dim, lax.axis_size(far)), near, dim + 1)
    return jnp.sum(lax.all_to_all(own, far, 0, 0, tiled=True), axis=0)


def total_of(shard, axes):
    lines = shard.reshape(-1, shard.shape[-1])
    padded = padded_to(lines, lax.axis_size(axes[0]) * lax.axis_size(axes[1]))
    whole = gather_axes(summed_rows(padded, axes, 0), axes, 0)
    return lax.slice_in_dim(whole, 0, len(lines)).reshape(shard.shape)


def silu_slope(pre_act):
    sigmoid_v = jax.nn.sigmoid(pre_act)
    return sigmoid_v * (1.0 + pre_act * (1.0 - sigmoid_v))


def body(
    node_state,
    edge_state,
    senders,
    receivers,
    send_index,
    cotangent,
    w_edge,
    w_node,
    error_memory,
    warm_q,
):
    highest = lax.Precision.HIGHEST
    node_block = node_state[0]
    edge_block = edge_state[0]
    features = node_block.shape[1]
    node_count = node_block.shape[0]
    partitions = lax.axis_size(GRAPH)
    outgoing = node_block[send_index[0, 0]].reshape(partitions, -1, features)
    incoming = lax.all_to_all(outgoing, GRAPH, split_axis=0, concat_axis=0, tiled=True)
    lookup = jnp.concatenate([node_block, incoming.reshape(-1, features)], axis=0)
    sender_rows = lookup[senders[0]]
    receiver_rows = node_block[receivers[0]]
    edge_pre = jnp.dot(edge_block, w_edge[:features], preferred_element_type=jnp.float32)
    edge_pre = edge_pre + jnp.dot(
        sender_rows, w_edge[features : 2 * features], preferred_element_type=jnp.float32
    )
    edge_pre = edge_pre + jnp.dot(
        receiver_rows, w_edge[2 * features :], preferred_element_type=jnp.float32
    )
    edge_new = (edge_block.astype(jnp.float32) + jax.nn.silu(edge_pre)).astype(jnp.bfloat16)
    incidence = (receivers[0][None, :] == jnp.arange(node_count, dtype=jnp.int32)[:, None]).astype(
        jnp.bfloat16
    )
    aggregate = jnp.dot(incidence, edge_new, preferred_element_type=jnp.float32).astype(
        jnp.bfloat16
    )
    node_pre = jnp.dot(node_block, w_node[:features], preferred_element_type=jnp.float32)
    node_pre = node_pre + jnp.dot(aggregate, w_node[features:], preferred_element_type=jnp.float32)
    new_block = (node_block.astype(jnp.float32) + jax.nn.silu(node_pre)).astype(jnp.bfloat16)
    node_delta = (cotangent[0].astype(jnp.float32) * silu_slope(node_pre)).astype(jnp.bfloat16)
    grad_top = jnp.einsum("nk,nj->kj", node_block, node_delta, preferred_element_type=jnp.float32)
    grad_low = jnp.einsum("nk,nj->kj", aggregate, node_delta, preferred_element_type=jnp.float32)
    gradient = jnp.concatenate([grad_top, grad_low], axis=0)
    mine = summed_on_arrival(gradient.astype(jnp.bfloat16), GRAPH, 0)
    matrix = mine + error_memory[0]
    local_left = jnp.dot(matrix, warm_q, precision=highest)
    own_left = over_copies(local_left, DP)
    gram = over_copies(jnp.dot(own_left.T, own_left, precision=highest), GRAPH)
    factor = jnp.linalg.cholesky(gram)
    ortho = lax.linalg.triangular_solve(
        factor, own_left, left_side=False, lower=True, transpose_a=True
    )
    right_part = jnp.dot(matrix.T, ortho, precision=highest)
    new_q = total_of(right_part, ("graph_0", ("graph_1", "dp_0", "dp_1"))) / lax.axis_size(DP)
    update = jnp.dot(ortho, new_q.T, precision=highest)
    new_error = matrix - update
    return (new_block[None], update, new_error[None], new_q)


def solution(mesh):
    finer = Mesh(mesh.devices.reshape(8, 4, 8, 2), ("graph_0", "graph_1", "dp_0", "dp_1"))
    placed = (
        P(DP, GRAPH, None),
        P(DP, GRAPH, None),
        P(DP, GRAPH),
        P(DP, GRAPH),
        P(DP, GRAPH, None),
        P(DP, GRAPH, None),
        P(),
        P(),
        P(DP, GRAPH, None),
        P(),
    )
    return jax.shard_map(
        body,
        mesh=finer,
        in_specs=placed,
        out_specs=(P(DP, GRAPH, None), P(GRAPH, None), P(DP, GRAPH, None), P()),
        check_vma=False,
    )
```

profile of v0, /device:TPU:1, one launch (start us, length us, event | category | flops | bytes accessed | tf_op | source)
XLA Modules:
  0.0 211.0 jit_solution(12772799770085606760)
XLA Ops:
  0.7 0.8 compare_select_fusion.2
  1.5 3.0 %gather_fusion = bf16[256,512]{1,0:T(8,128)(2,1)} fusion(bf16[512,512]{1,0:T(8,128)(2,1)} %bitcast.90, s32[1024]{0:T(1024)S(1)} %pad_clamp_fusion), kind=kCustom, calls=%fused_computation | custom fusion | bytes 525312 | tf_op jit(solution)/shard_map/gather | solution.py:95
  4.5 13.7 %all-to-all-start = ((bf16[32,8,512]{2,1,0:T(8,128)(2,1)}), bf16[32,8,512]{2,1,0:T(8,128)(2,1)S(1)}, u32[]{:S(2)}, u32[]{:S(2)}) async-start(bf16[32,8,512]{2,1,0:T(8,128)(2,1)} %bitcast.5), calls=%async_computation | async-start | bytes 524288 | tf_op jit(solution)/shard_map/all_to_all | solution.py:96
  18.3 1.4 fusion.13
  19.7 9.2 %gather_fusion.2 = bf16[2048,512]{1,0:T(8,128)(2,1)} fusion(bf16[512,512]{1,0:T(8,128)(2,1)S(1)} %bitcast.91, s32[2048]{0:T(1024)S(1)} %broadcast_clamp_fusion), kind=kCustom, calls=%fused_computation.2 | custom fusion | bytes 4202496 | tf_op jit(solution)/shard_map/gather | solution.py:99
  28.9 4.2 %fusion.1 = f32[2048,512]{1,0:T(8,128)} fusion(bf16[1,2048,512]{2,1,0:T(8,128)(2,1)S(1)} %copy-done.2, bf16[1536,512]{1,0:T(8,128)(2,1)} %param.16), kind=kOutput, calls=%fused_computation.6 | convolution fusion | flops 1073741824 | bytes 6815744 | tf_op jit(solution)/shard_map/dot_general | solution.py:100
  33.1 0.7 copy-done.4
  33.8 1.0 pad_maximum_fusion.1
  34.8 7.5 %gather_fusion.1 = bf16[2048,512]{1,0:T(8,128)(2,1)S(1)} fusion(bf16[768,512]{1,0:T(8,128)(2,1)S(1)} %pad_maximum_fusion.1, s32[2048]{0:T(1024)S(1)} %broadcast_clamp_fusion.1), kind=kCustom, calls=%fused_computation.1 | custom fusion | bytes 4202496 | tf_op jit(solution)/shard_map/gather | solution.py:98
  42.4 4.3 %fusion.10 = f32[2048,512]{1,0:T(8,128)} fusion(bf16[2048,512]{1,0:T(8,128)(2,1)S(1)} %gather_fusion.1, bf16[1536,512]{1,0:T(8,128)(2,1)} %param.16), kind=kOutput, calls=%fused_computation.24 | convolution fusion | flops 1073741824 | bytes 6815744 | tf_op jit(solution)/shard_map/dot_general | solution.py:101
  46.7 9.0 %fusion.4 = bf16[512,512]{1,0:T(8,128)(2,1)} fusion(s32[2048]{0:T(1024)S(1)} %bitcast.100, f32[2048,512]{1,0:T(8,128)} %fusion.1, f32[2048,512]{1,0:T(8,128)} %fusion.10, bf16[2048,512]{1,0:T(8,128)(2,1)} %gather_fusion.2, bf16[1,2048,512]{2,1,0:T(8,128)(2,1)} %param.11, bf16[1536,512]{1,0:T(8,128)(2,1)} %param.16), kind=kOutput, calls=%fused_computation.11 | convolution fusion | flops 2158231552 | bytes 13639680 | tf_op jit(solution)/shard_map/dot_general | solution.py:111
  55.6 2.8 %fusion.6 = (bf16[512,512]{1,0:T(8,128)(2,1)S(1)}, bf16[1,512,512]{2,1,0:T(8,128)(2,1)}) fusion(bf16[1,512,512]{2,1,0:T(8,128)(2,1)S(1)} %copy-done.12, bf16[1,512,512]{2,1,0:T(8,128)(2,1)S(1)} %copy-done.1, f32[512,512]{1,0:T(8,128)S(1)} %copy-done.3, bf16[512,512]{1,0:T(8,128)(2,1)} %fusion.4, bf16[1024,512]{1,0:T(8,128)(2,1)S(1)} %copy-done.9), kind=kOutput, calls=%fused_computation.18 | convolution fusion | flops 272367616 | bytes 4194304 | tf_op jit(solution)/shard_map/dot_general | solution.py:115
  59.5 35.0 %all_to_all.40 = bf16[32,32,512]{2,1,0:T(8,128)(2,1)S(1)} all-to-all(bf16[32,32,512]{2,1,0:T(8,128)(2,1)S(1)} %bitcast.93), channel_id=1, replica_groups=mesh['graph_0'=8,'graph_1'=4,'dp_0'=8,'dp_1'=2] {'graph_0','graph_1'}, dimensions={0} | all-to-all | bytes 2097152 | tf_op jit(solution)/shard_map/all_to_all | solution.py:18
  95.1 18.9 %all_to_all.41 = f32[16,1,2048]{2,1,0:T(1,128)S(1)} all-to-all(f32[16,1,2048]{2,1,0:T(1,128)S(1)} %reshape.158), channel_id=1, replica_groups=mesh['graph_0'=8,'graph_1'=4,'dp_0'=8,'dp_1'=2] {'dp_0','dp_1'}, dimensions={0} | all-to-all | bytes 262144 | tf_op jit(solution)/shard_map/all_to_all | solution.py:24
  114.0 0.5 broadcast.122
  114.5 0.9 reduce.8
  116.0 1.4 reshape.160
  117.4 5.5 %all-to-all-start.3 = ((f32[32,1,4096]{2,1,0:T(1,128)}), f32[32,1,4096]{2,1,0:T(1,128)S(1)}, u32[]{:S(2)}, u32[]{:S(2)}) async-start(f32[32,1,4096]{2,1,0:T(1,128)} %reshape.160), calls=%async_computation.3 | async-start | bytes 1048576 | tf_op jit(solution)/shard_map/all_to_all | solution.py:24
  123.0 16.6 %all-to-all-done.3 = f32[32,1,4096]{2,1,0:T(1,128)S(1)} async-done(((f32[32,1,4096]{2,1,0:T(1,128)}), f32[32,1,4096]{2,1,0:T(1,128)S(1)}, u32[]{:S(2)}, u32[]{:S(2)}) %all-to-all-start.3) | async-done | bytes 524320 | tf_op jit(solution)/shard_map/all_to_all | solution.py:24
  139.7 1.9 reduce.9
  142.2 5.8 %cholesky.16 = f32[64,64]{1,0:T(8,128)S(1)} custom-call(f32[64,64]{1,0:T(8,128)S(1)} %fusion.20), custom_call_target="Cholesky" | custom-call | tf_op jit(solution)/shard_map/jit(cholesky)/cholesky | solution.py:126
  148.1 0.6 compare_reduce_fusion
  148.7 0.7 fusion.17
  149.4 4.9 %custom-call.6 = f32[1,64,64]{1,2,0:T(8,128)S(1)} custom-call(f32[1,64,64]{2,1,0:T(8,128)S(1)} %fusion.17), custom_call_target="InvertDiagBlocksLowerTriangular" | custom-call | tf_op jit(solution)/shard_map/triangular_solve | solution.py:127
  154.4 0.6 convolution_bitcast_fusion
  155.4 16.8 %all_to_all.42 = f32[64,1,512]{2,1,0:T(1,128)S(1)} all-to-all(f32[64,1,512]{2,1,0:T(1,128)S(1)} %reshape.162), channel_id=1, replica_groups=mesh['graph_0'=8,'graph_1'=4,'dp_0'=8,'dp_1'=2] {'graph_1','dp_0','dp_1'}, dimensions={0} | all-to-all | bytes 262144 | tf_op jit(solution)/shard_map/all_to_all | solution.py:55
  172.2 1.0 reduce.10
  173.3 8.9 %all_to_all.43 = f32[8,1,64]{2,1,0:T(1,128)S(1)} all-to-all(f32[8,1,64]{2,1,0:T(1,128)S(1)} %bitcast.98), channel_id=1, replica_groups=mesh['graph_0'=8,'graph_1'=4,'dp_0'=8,'dp_1'=2] {'graph_0'}, dimensions={0} | all-to-all | bytes 4096 | tf_op jit(solution)/shard_map/all_to_all | solution.py:62
  182.3 8.9 %all_to_all.44 = f32[8,1,64]{2,1,0:T(1,128)S(1)} all-to-all(f32[8,1,64]{2,1,0:T(1,128)S(1)} %broadcast_in_dim.19), channel_id=1, replica_groups=mesh['graph_0'=8,'graph_1'=4,'dp_0'=8,'dp_1'=2] {'graph_0'}, dimensions={0} | all-to-all | bytes 4096 | tf_op jit(solution)/shard_map/all_to_all | solution.py:24
  191.4 17.3 %all_to_all.45 = f32[64,1,512]{2,1,0:T(1,128)S(1)} all-to-all(f32[64,1,512]{2,1,0:T(1,128)S(1)} %reshape.164), channel_id=1, replica_groups=mesh['graph_0'=8,'graph_1'=4,'dp_0'=8,'dp_1'=2] {'graph_1','dp_0','dp_1'}, dimensions={0} | all-to-all | bytes 262144 | tf_op jit(solution)/shard_map/all_to_all | solution.py:24
  208.7 1.0 reduce.11
  210.3 0.6 subtract_bitcast_fusion
  (65 shorter events, 4.4 us)
Async XLA Ops:
  0.6 94.0 %copy-start = (f32[512,64]{0,1:T(8,128)S(1)}, f32[512,64]{0,1:T(8,128)}, u32[]{:S(2)}) copy-start(f32[512,64]{0,1:T(8,128)} %param.19) | copy-start | bytes 393220
  0.6 17.7 %copy-start.1 = (bf16[1,512,512]{2,1,0:T(8,128)(2,1)S(1)}, bf16[1,512,512]{2,1,0:T(8,128)(2,1)}, u32[]{:S(2)}) copy-start(bf16[1,512,512]{2,1,0:T(8,128)(2,1)} %param.10) | copy-start | bytes 1572868
  0.7 17.6 %copy-start.10 = (s32[1,2048]{1,0:T(1,128)S(1)}, s32[1,2048]{1,0:T(1,128)}, u32[]{:S(2)}) copy-start(s32[1,2048]{1,0:T(1,128)} %param.12) | copy-start | bytes 24580
  0.7 17.6 %copy-start.11 = (s32[1,2048]{1,0:T(1,128)S(1)}, s32[1,2048]{1,0:T(1,128)}, u32[]{:S(2)}) copy-start(s32[1,2048]{1,0:T(1,128)} %param.13) | copy-start | bytes 24580
  0.7 17.6 %copy-start.8 = (bf16[1024,512]{1,0:T(8,128)(2,1)S(1)}, bf16[1024,512]{1,0:T(8,128)(2,1)}, u32[]{:S(2)}) copy-start(bf16[1024,512]{1,0:T(8,128)(2,1)} %param.17) | copy-start | bytes 3145732
  4.5 28.6 %all-to-all-start = ((bf16[32,8,512]{2,1,0:T(8,128)(2,1)}), bf16[32,8,512]{2,1,0:T(8,128)(2,1)S(1)}, u32[]{:S(2)}, u32[]{:S(2)}) async-start(bf16[32,8,512]{2,1,0:T(8,128)(2,1)} %bitcast.5), calls=%async_computation | async-start | bytes 524288 | tf_op jit(solution)/shard_map/all_to_all | solution.py:96
  19.7 9.2 %copy-start.2 = (bf16[1,2048,512]{2,1,0:T(8,128)(2,1)S(1)}, bf16[1,2048,512]{2,1,0:T(8,128)(2,1)}, u32[]{:S(2)}) copy-start(bf16[1,2048,512]{2,1,0:T(8,128)(2,1)} %param.11) | copy-start | bytes 6291460
  33.1 0.7 copy-start.4
  46.6 9.0 %copy-start.3 = (f32[512,512]{1,0:T(8,128)S(1)}, f32[512,512]{1,0:T(8,128)}, u32[]{:S(2)}) copy-start(f32[512,512]{1,0:T(8,128)} %fusion.13) | copy-start | bytes 3145732
  46.7 9.0 %copy-start.9 = (bf16[1024,512]{1,0:T(8,128)(2,1)S(1)}, bf16[1024,512]{1,0:T(8,128)(2,1)}, u32[]{:S(2)}) copy-start(bf16[1024,512]{1,0:T(8,128)(2,1)} %param.17) | copy-start | bytes 3145732
  46.7 9.0 %copy-start.12 = (bf16[1,512,512]{2,1,0:T(8,128)(2,1)S(1)}, bf16[1,512,512]{2,1,0:T(8,128)(2,1)}, u32[]{:S(2)}) copy-start(bf16[1,512,512]{2,1,0:T(8,128)(2,1)} %param.15) | copy-start | bytes 1572868
  55.6 2.8 %copy-start.13 = (bf16[512,512]{1,0:T(8,128)(2,1)S(1)}, bf16[512,512]{1,0:T(8,128)(2,1)}, u32[]{:S(2)}) copy-start(bf16[512,512]{1,0:T(8,128)(2,1)} %fusion.4) | copy-start | bytes 1572868
  59.5 35.2 %copy-start.5 = (f32[1,32,512]{2,1,0:T(8,128)S(1)}, f32[1,32,512]{2,1,0:T(8,128)}, u32[]{:S(2)}) copy-start(f32[1,32,512]{2,1,0:T(8,128)} %param.18) | copy-start | bytes 196612
  117.4 22.2 %all-to-all-start.3 = ((f32[32,1,4096]{2,1,0:T(1,128)}), f32[32,1,4096]{2,1,0:T(1,128)S(1)}, u32[]{:S(2)}, u32[]{:S(2)}) async-start(f32[32,1,4096]{2,1,0:T(1,128)} %reshape.160), calls=%async_computation.3 | async-start | bytes 1048576 | tf_op jit(solution)/shard_map/all_to_all | solution.py:24
  210.1 0.9 copy-start.6
  210.3 0.7 copy-start.7
where the time goes:
time: 212 us; the launch traced here: 211 us
  blocking collectives  106 us (50%)
  local copies, waits for them, and re-layouts  24.5 us (12%)
  matrix products  24 us (11%)
  other arithmetic  19.8 us (9%)
  starting transfers between devices  19.2 us (9%)
  waiting for transfers between devices  16.6 us (8%)
    all_to_all x3, blocking collectives, from_everyone(): lax.all_to_all(jnp.broadcast_to(shard[None], (count, *shard.shape)), axis...  45.1 us
    all_to_all x1, blocking collectives, summed_on_arrival(): lax.all_to_all(cut_along(shard, dim, count), axis, 0, 0, tiled=True)  35 us
    all_to_all x1, blocking collectives, sum_at_owner(): lax.all_to_all(pieces, axis, split_axis=0, concat_axis=0, tiled=True)  16.8 us
    all_to_all x1, waiting for transfers between devices, from_everyone(): lax.all_to_all(jnp.broadcast_to(shard[None], (count, *shard.shape)), axis...  16.6 us
    all_to_all x1, starting transfers between devices, body(): lax.all_to_all(outgoing, GRAPH, split_axis=0, concat_axis=0, tiled=True)  13.7 us
    gather x1, local copies, waits for them, and re-layouts, body(): receiver_rows = node_block[receivers[0]]  9.16 us
    dot_general x1, matrix products, body(): jnp.dot(incidence, edge_new, preferred_element_type=jnp.float32)  8.96 us
    all_to_all x1, blocking collectives, summed_rows(): return jnp.sum(lax.all_to_all(own, far, 0, 0, tiled=True), axis=0)  8.92 us
  transfers between devices with their start and end apart: 2, of which 1 were waited for; matrix products, arithmetic and copies ran while one was open for 7% of the time, Pallas kernels for 0%

commit v1 on v0

v1 whole, which is shorter than its diff:
```python
import functools

import jax
import jax.numpy as jnp
from jax import lax
from jax.experimental import pallas as pl
from jax.experimental.pallas import tpu as pltpu
from jax.sharding import Mesh
from jax.sharding import PartitionSpec as P

AXES = ("graph_0", "graph_1", "dp_0", "dp_1")
GRAPH = AXES[:2]
DP = AXES[2:]
MESH = pl.DeviceIdType.MESH
BF = jnp.bfloat16
F32 = jnp.float32
HIGH = lax.Precision.HIGHEST
LANE = 128


def mm(a, b, dims=((1,), (0,)), precision=None):
    return lax.dot_general(a, b, (dims, ((), ())), precision=precision, preferred_element_type=F32)


def sigmoid(v):
    return 0.5 + 0.5 * jnp.tanh(0.5 * v)


def column(row):
    eye = lax.broadcasted_iota(jnp.int32, (LANE, LANE), 0) == lax.broadcasted_iota(
        jnp.int32, (LANE, LANE), 1
    )
    return jnp.sum(jnp.where(eye, row, 0.0), axis=1, keepdims=True)


def one_hot(col, width, base=0):
    lanes = lax.broadcasted_iota(jnp.int32, (col.shape[0], width), 1) + base
    return jnp.where(lanes.astype(F32) == col, 1.0, 0.0).astype(BF)


def inverse_factor(gram):
    n = gram.shape[0]
    rows = lax.broadcasted_iota(jnp.int32, (n, 1), 0)
    eye = jnp.where(
        lax.broadcasted_iota(jnp.int32, (n, n), 0) == lax.broadcasted_iota(jnp.int32, (n, n), 1),
        1.0,
        0.0,
    ).astype(F32)
    work = jnp.concatenate([gram, eye], axis=1)
    for k in range(n - 1):
        pivot = work[k : k + 1, :]
        scaled = pivot / pivot[:, k : k + 1]
        work = work - jnp.where(rows > k, work[:, k : k + 1], 0.0) * scaled
    diagonal = jnp.sum(work[:, :n] * eye, axis=1, keepdims=True)
    return work[:, n:] / jnp.sqrt(diagonal)


def kernel(
    sizes,
    node_hbm,
    edge_hbm,
    senders_hbm,
    receivers_hbm,
    send_hbm,
    cot_hbm,
    w_edge_hbm,
    w_node_hbm,
    error_hbm,
    warm_hbm,
    new_nodes_hbm,
    update_ref,
    new_error_ref,
    new_q_ref,
    node,
    edge,
    senders,
    receivers,
    send_index,
    cot,
    w_edge,
    w_node,
    error,
    warm,
    load_sem,
    store_sem,
    halo_out,
    halo_in,
    own_p,
    own_r,
    halo_p,
    pre,
    pick_halo,
    incidence,
    total,
    new_block,
    delta,
    inputs_t,
    grad_a,
    grad_b,
    ax_in,
    ax_sum,
    az_in,
    bz_in,
    b_sum,
    bx_in,
    matrix,
    dp_out,
    dp_in,
    z_out,
    z_in,
    x_out,
    x_in,
    q_out,
    q_in,
    halo_s,
    halo_r,
    ax_s,
    ax_r,
    az_s,
    az_r,
    bz_s,
    bz_r,
    bx_s,
    bx_r,
    dp_s,
    dp_r,
    z_s,
    z_r,
    x_s,
    x_r,
    q_s,
    q_r,
):
    nz, nx, ny, nc, cut, tile = sizes
    ng, nd = nz * nx, ny * nc
    count, width = node.shape
    edges = edge.shape[0]
    tiles = edges // tile
    chunks = tile // LANE
    z, x = lax.axis_index(AXES[0]), lax.axis_index(AXES[1])
    y, c = lax.axis_index(AXES[2]), lax.axis_index(AXES[3])
    part = z * nx + x
    group = y * nc + c

    def on_graph(index):
        return (index // nx, lax.rem(index, nx), y, c)

    def on_dp(index):
        return (z, x, index // nc, lax.rem(index, nc))

    def on_z(index):
        return (index, x, y, c)

    def on_x(index):
        return (z, index, y, c)

    def remote(src, dst, send, recv, device):
        return pltpu.make_async_remote_copy(
            src_ref=src,
            dst_ref=dst,
            send_sem=send,
            recv_sem=recv,
            device_id=device,
            device_id_type=MESH,
        )

    loads = [
        pltpu.make_async_copy(src, dst, load_sem.at[i])
        for i, (src, dst) in enumerate(
            [
                (send_hbm, send_index),
                (node_hbm, node),
                (receivers_hbm, receivers),
                (senders_hbm, senders),
                (w_edge_hbm, w_edge),
                (edge_hbm, edge),
                (w_node_hbm, w_node),
                (cot_hbm, cot),
                (error_hbm, error),
                (warm_hbm, warm),
            ]
        )
    ]
    for load in loads:
        load.start()

    barrier = pltpu.get_barrier_semaphore()

    @pl.loop(1, ng)
    def _(o):
        pl.semaphore_signal(
            barrier, inc=1, device_id=on_graph(lax.rem(part + o, ng)), device_id_type=MESH
        )

    @pl.loop(1, nd)
    def _(o):
        pl.semaphore_signal(
            barrier, inc=1, device_id=on_dp(lax.rem(group + o, nd)), device_id_type=MESH
        )

    loads[0].wait()
    loads[1].wait()
    half = width // 2
    peer = send_index.shape[0] * LANE // ng
    per = LANE // peer
    for i in range(send_index.shape[0]):
        col = column(send_index[i : i + 1, :].astype(F32))
        rows = mm(one_hot(col, count), node[...])
        pair = jnp.concatenate(
            [
                rows[:, :half].reshape(per, peer, half),
                rows[:, half:].reshape(per, peer, half),
            ],
            axis=1,
        )
        halo_out[i * per : (i + 1) * per] = pair.astype(BF)
    halo_in[pl.ds(part, 1)] = halo_out[pl.ds(part, 1)]

    pl.semaphore_wait(barrier, ng - 1 + nd - 1)

    def halo_copy(o):
        to = lax.rem(part + o, ng)
        return remote(
            halo_out.at[to], halo_in.at[part], halo_s.at[o - 1], halo_r.at[o - 1], on_graph(to)
        )

    @pl.loop(1, ng)
    def _(o):
        halo_copy(o).start()

    loads[2].wait()
    loads[3].wait()
    loads[4].wait()
    own_p[...] = mm(node[...], w_edge[width : 2 * width, :]).astype(BF)
    own_r[...] = mm(node[...], w_edge[2 * width :, :]).astype(BF)
    loads[5].wait()

    @pl.loop(0, tiles)
    def _(t):
        at = pl.ds(pl.multiple_of(t * tile, tile), tile)
        from_col = jnp.concatenate(
            [
                column(senders[pl.ds(t * chunks + j, 1), :].astype(F32))
                for j in range(chunks)
            ],
            axis=0,
        )
        to_rows = [receivers[pl.ds(t * chunks + j, 1), :].astype(F32) for j in range(chunks)]
        to_col = jnp.concatenate([column(row) for row in to_rows], axis=0)
        value = mm(edge[at, :], w_edge[:width, :])
        value = value + mm(one_hot(from_col, count), own_p[...])
        value = value + mm(one_hot(to_col, count), own_r[...])
        pre[at, :] = value
        pick_halo[at, :] = one_hot(from_col, halo_p.shape[0], count)
        ids = lax.broadcasted_iota(jnp.int32, (count, LANE), 0).astype(F32)
        for j, row in enumerate(to_rows):
            incidence[t, :, j * LANE : (j + 1) * LANE] = jnp.where(ids == row, 1.0, 0.0).astype(BF)

    inputs_t[:width, :] = node[...].astype(F32).T.astype(BF)

    @pl.loop(1, ng)
    def _(o):
        halo_copy(o).wait()

    flat = halo_in[...].reshape(ng * 2 * peer, half)
    left_half = mm(flat, w_edge[width : width + half, :]).reshape(ng, 2, peer, width)
    right_half = mm(flat, w_edge[width + half : 2 * width, :]).reshape(ng, 2, peer, width)
    halo_p[...] = (left_half[:, 0] + right_half[:, 1]).reshape(ng * peer, width).astype(BF)

    total[...] = jnp.zeros_like(total)

    @pl.loop(0, tiles)
    def _(t):
        at = pl.ds(pl.multiple_of(t * tile, tile), tile)
        value = pre[at, :] + mm(pick_halo[at, :], halo_p[...])
        fresh = (edge[at, :].astype(F32) + value * sigmoid(value)).astype(BF)
        total[...] += mm(incidence[t], fresh)

    loads[6].wait()
    loads[7].wait()
    summed = total[...].astype(BF)
    node_pre = mm(node[...], w_node[:width, :]) + mm(summed, w_node[width:, :])
    gate = sigmoid(node_pre)
    delta[...] = (cot[...].astype(F32) * (gate * (1.0 + node_pre * (1.0 - gate)))).astype(BF)
    new_block[...] = (node[...].astype(F32) + node_pre * gate).astype(BF)
    store = pltpu.make_async_copy(new_block, new_nodes_hbm, store_sem.at[0])
    store.start()
    inputs_t[width:, :] = total[...].T.astype(BF)

    share = 2 * width // ng
    step = min(nz, max(1, 256 // (nx * share)))

    @pl.loop(0, nz // step)
    def _(i):
        lines = step * nx * share
        grad = mm(inputs_t[pl.ds(pl.multiple_of(i * lines, lines), lines), :], delta[...])
        at = pl.ds(i * step, step)
        grad_a[at] = grad[:, :cut].reshape(step, nx, share, cut).astype(BF)
        grad_b[at] = grad[:, cut:].reshape(step, nx, share, width - cut).astype(BF)

    z_order = sorted(range(1, nz), key=lambda o: -min(o, nz - o))
    x_order = sorted(range(1, nx), key=lambda o: -min(o, nx - o))
    turns = z_order + [0]

    def z_at(o):
        return lax.rem(z + o, nz)

    def x_at(o):
        return lax.rem(x + o, nx)

    bz = {
        o: remote(
            grad_b.at[z_at(o)], bz_in.at[o - 1], bz_s.at[o - 1], bz_r.at[o - 1], on_z(z_at(o))
        )
        for o in z_order
    }
    ax = {
        (t, o): remote(
            grad_a.at[z_at(t), x_at(o)],
            ax_in.at[o - 1, t],
            ax_s.at[o - 1, t],
            ax_r.at[o - 1, t],
            on_x(x_at(o)),
        )
        for t in turns
        for o in x_order
    }
    az = {
        o: remote(ax_sum.at[o], az_in.at[o - 1], az_s.at[o - 1], az_r.at[o - 1], on_z(z_at(o)))
        for o in z_order
    }
    bx = {
        o: remote(
            b_sum.at[x_at(o)], bx_in.at[o - 1], bx_s.at[o - 1], bx_r.at[o - 1], on_x(x_at(o))
        )
        for o in x_order
    }
    for copy in bz.values():
        copy.start()
    for copy in ax.values():
        copy.start()
    for t in turns:
        value = grad_a[z_at(t), x].astype(F32)
        for o in x_order:
            ax[t, o].wait_recv()
            value = value + ax_in[o - 1, t].astype(F32)
        if t:
            ax_sum[t] = value.astype(BF)
            az[t].start()
        else:
            own_a = value
    value = grad_b[z].astype(F32)
    for o in z_order:
        bz[o].wait_recv()
        value = value + bz_in[o - 1].astype(F32)
    b_sum[...] = value.astype(BF)
    for copy in bx.values():
        copy.start()
    own_b = b_sum[x].astype(F32)
    for o in x_order:
        bx[o].wait_recv()
        own_b = own_b + bx_in[o - 1].astype(F32)
    for o in z_order:
        az[o].wait_recv()
        own_a = own_a + az_in[o - 1].astype(F32)
    loads[8].wait()
    loads[9].wait()
    matrix[:, :cut] = own_a + error[:, :cut]
    matrix[:, cut:] = own_b + error[:, cut:]

    rank = warm.shape[0]
    pack = LANE // rank
    blocks = width // LANE
    piece = LANE // nd
    local = mm(matrix[...], warm[...], ((1,), (1,)), HIGH)
    packed = jnp.concatenate([local[: share // 2], local[share // 2 :]], axis=1)
    turned = jnp.concatenate(
        [matrix[:, q * LANE : (q + 1) * LANE] for q in range(blocks)], axis=0
    ).T
    dp_out[:, :piece, :] = turned.reshape(nd, piece, LANE)
    dp_out[:, piece:, :] = jnp.broadcast_to(packed[None], (nd, *packed.shape))
    dp_in[pl.ds(group, 1)] = dp_out[pl.ds(group, 1)]

    def dp_copy(o):
        to = lax.rem(group + o, nd)
        return remote(dp_out.at[to], dp_in.at[group], dp_s.at[o - 1], dp_r.at[o - 1], on_dp(to))

    @pl.loop(1, nd)
    def _(o):
        dp_copy(o).start()

    @pl.loop(1, nd)
    def _(o):
        dp_copy(o).wait()

    arrived = jnp.sum(dp_in[...], axis=0)
    columns, packed = arrived[:piece], arrived[piece:]
    left = jnp.concatenate([packed[:, :rank], packed[:, rank:]], axis=0)
    gram = mm(left, left, ((0,), (0,)), HIGH)
    twice = jnp.concatenate([left, left], axis=1)
    spread = jnp.concatenate([twice] * blocks, axis=0)
    owner = lax.broadcasted_iota(jnp.int32, (LANE, LANE), 0) // share
    side = lax.broadcasted_iota(jnp.int32, (LANE, LANE), 1) // rank
    halves = blocks // pack
    for h in range(halves):
        chosen = jnp.where(owner == pack * h + side, spread, 0.0)
        z_out[h * piece : (h + 1) * piece, :] = mm(columns, chosen, precision=HIGH)
    z_out[halves * piece :, :] = jnp.concatenate([gram[: rank // 2], gram[rank // 2 :]], axis=1)

    z_in[pl.ds(z, 1)] = z_out[...][None]
    zs = {
        o: remote(z_out, z_in.at[z], z_s.at[o - 1], z_r.at[o - 1], on_z(z_at(o)))
        for o in z_order
    }
    for copy in zs.values():
        copy.start()
    for copy in zs.values():
        copy.wait()
    x_out[...] = jnp.sum(z_in[...], axis=0)
    x_in[pl.ds(x, 1)] = x_out[...][None]
    xs = {
        o: remote(x_out, x_in.at[x], x_s.at[o - 1], x_r.at[o - 1], on_x(x_at(o)))
        for o in x_order
    }
    for copy in xs.values():
        copy.start()
    for copy in xs.values():
        copy.wait()
    both = jnp.sum(x_in[...], axis=0)

    q_out[...] = both[: halves * piece]
    q_in[pl.ds(group, 1)] = q_out[...][None]

    def q_copy(o):
        to = lax.rem(group + o, nd)
        return remote(q_out, q_in.at[group], q_s.at[o - 1], q_r.at[o - 1], on_dp(to))

    @pl.loop(1, nd)
    def _(o):
        q_copy(o).start()

    packed = both[halves * piece :]
    gram = jnp.concatenate([packed[:, :rank], packed[:, rank:]], axis=0)
    inverse = inverse_factor(gram)
    ortho = mm(left, inverse, ((1,), (1,)), HIGH)

    @pl.loop(1, nd)
    def _(o):
        q_copy(o).wait()

    for h in range(halves):
        right = q_in[:, h * piece : (h + 1) * piece, :].reshape(LANE, LANE)
        for side in range(pack):
            q = h * pack + side
            at = slice(q * LANE, (q + 1) * LANE)
            new_q = mm(inverse, right[:, side * rank : (side + 1) * rank], ((1,), (1,)), HIGH) / nd
            new_q_ref[:, at] = new_q
            update = mm(ortho, new_q, precision=HIGH)
            update_ref[:, at] = update
            new_error_ref[:, at] = matrix[:, at] - update

    for copies in (bz, ax, az, bx):
        for copy in copies.values():
            copy.wait_send()
    store.wait()


def layer(
    sizes,
    node_state,
    edge_state,
    senders,
    receivers,
    send_index,
    cotangent,
    w_edge,
    w_node,
    error_memory,
    warm_q,
):
    nz, nx, ny, nc, cut, tile = sizes
    ng, nd = nz * nx, ny * nc
    count, width = node_state.shape[1:]
    edges = edge_state.shape[1]
    rank = warm_q.shape[1]
    share = 2 * width // ng
    halo = send_index.shape[-1]
    peer = halo // ng
    piece = LANE // nd
    halves = width * rank // LANE // LANE
    hbm = pl.BlockSpec(memory_space=pltpu.MemorySpace.HBM)
    vmem = pl.BlockSpec(memory_space=pltpu.VMEM)
    dma = pltpu.SemaphoreType.DMA
    exchange = halves * piece + rank // 2
    new_block, update, new_error, new_q = pl.pallas_call(
        functools.partial(kernel, sizes),
        out_shape=(
            jax.ShapeDtypeStruct((count, width), BF),
            jax.ShapeDtypeStruct((share, width), F32),
            jax.ShapeDtypeStruct((share, width), F32),
            jax.ShapeDtypeStruct((rank, width), F32),
        ),
        in_specs=[hbm] * 10,
        out_specs=(hbm, vmem, vmem, vmem),
        scratch_shapes=[
            pltpu.VMEM((count, width), BF),
            pltpu.VMEM((edges, width), BF),
            pltpu.VMEM((edges // LANE, LANE), jnp.int32),
            pltpu.VMEM((edges // LANE, LANE), jnp.int32),
            pltpu.VMEM((halo // LANE, LANE), jnp.int32),
            pltpu.VMEM((count, width), BF),
            pltpu.VMEM((3 * width, width), BF),
            pltpu.VMEM((2 * width, width), BF),
            pltpu.VMEM((share, width), F32),
            pltpu.VMEM((rank, width), F32),
            dma((10,)),
            dma((1,)),
            pltpu.VMEM((ng, 2 * peer, width // 2), BF),
            pltpu.VMEM((ng, 2 * peer, width // 2), BF),
            pltpu.VMEM((count, width), BF),
            pltpu.VMEM((count, width), BF),
            pltpu.VMEM((halo, width), BF),
            pltpu.VMEM((edges, width), F32),
            pltpu.VMEM((edges, halo), BF),
            pltpu.VMEM((edges // tile, count, tile), BF),
            pltpu.VMEM((count, width), F32),
            pltpu.VMEM((count, width), BF),
            pltpu.VMEM((count, width), BF),
            pltpu.VMEM((2 * width, count), BF),
            pltpu.VMEM((nz, nx, share, cut), BF),
            pltpu.VMEM((nz, nx, share, width - cut), BF),
            pltpu.VMEM((nx - 1, nz, share, cut), BF),
            pltpu.VMEM((nz, share, cut), BF),
            pltpu.VMEM((nz - 1, share, cut), BF),
            pltpu.VMEM((nz - 1, nx, share, width - cut), BF),
            pltpu.VMEM((nx, share, width - cut), BF),
            pltpu.VMEM((nx - 1, share, width - cut), BF),
            pltpu.VMEM((share, width), F32),
            pltpu.VMEM((nd, piece + share // 2, LANE), F32),
            pltpu.VMEM((nd, piece + share // 2, LANE), F32),
            pltpu.VMEM((exchange, LANE), F32),
            pltpu.VMEM((nz, exchange, LANE), F32),
            pltpu.VMEM((exchange, LANE), F32),
            pltpu.VMEM((nx, exchange, LANE), F32),
            pltpu.VMEM((halves * piece, LANE), F32),
            pltpu.VMEM((nd, halves * piece, LANE), F32),
            dma((ng - 1,)),
            dma((ng - 1,)),
            dma((nx - 1, nz)),
            dma((nx - 1, nz)),
            dma((nz - 1,)),
            dma((nz - 1,)),
            dma((nz - 1,)),
            dma((nz - 1,)),
            dma((nx - 1,)),
            dma((nx - 1,)),
            dma((nd - 1,)),
            dma((nd - 1,)),
            dma((nz - 1,)),
            dma((nz - 1,)),
            dma((nx - 1,)),
            dma((nx - 1,)),
            dma((nd - 1,)),
            dma((nd - 1,)),
        ],
        compiler_params=pltpu.CompilerParams(
            collective_id=0, has_side_effects=True, vmem_limit_bytes=67043328
        ),
    )(
        node_state[0],
        edge_state[0],
        senders.reshape(-1, LANE),
        receivers.reshape(-1, LANE),
        send_index.reshape(-1, LANE),
        cotangent[0],
        w_edge,
        w_node,
        error_memory[0],
        warm_q.T,
    )
    return new_block[None], update, new_error[None], new_q.T


def build(finer, cut, tile):
    placed = (
        P(DP, GRAPH, None),
        P(DP, GRAPH, None),
        P(DP, GRAPH),
        P(DP, GRAPH),
        P(DP, GRAPH, None),
        P(DP, GRAPH, None),
        P(),
        P(),
        P(DP, GRAPH, None),
        P(),
    )
    sizes = (*(finer.shape[a] for a in AXES), cut, tile)
    return jax.shard_map(
        functools.partial(layer, sizes),
        mesh=finer,
        in_specs=placed,
        out_specs=(P(DP, GRAPH, None), P(GRAPH, None), P(DP, GRAPH, None), P()),
        check_vma=False,
    )


def solution(mesh):
    return build(Mesh(mesh.devices.reshape(8, 4, 8, 2), AXES), 384, 512)
```

time: 212 us -> 79.1 us (0.37)
  blocking collectives: 106 us -> 0 us
  Pallas kernels: 0 us -> 71.8 us
  matrix products: 24 us -> 0 us
  other arithmetic: 19.8 us -> 0 us
  starting transfers between devices: 19.2 us -> 0 us
  local copies, waits for them, and re-layouts: 24.5 us -> 6.38 us
  waiting for transfers between devices: 16.6 us -> 0 us
    all_to_all x6 -> x0, blocking collectives: 106 us -> none  [the longest x3 45.1 us: from_everyone(): lax.all_to_all(jnp.broadcast_to(shard[None], (count, *shard.shape)), axis...]
    pallas_call x0 -> x1, Pallas kernels: none -> 71.8 us  [layer(): pl.pallas_call(functools.partial(kernel, sizes), out_shape=(jax.ShapeDtyp...]
    dot_general x11 -> x0, matrix products: 23.9 us -> none  [the longest x1 8.96 us: body(): jnp.dot(incidence, edge_new, preferred_element_type=jnp.float32)]
    gather x3 -> x0, local copies, waits for them, and re-layouts: 19.7 us -> none  [the longest x1 9.16 us: body(): receiver_rows = node_block[receivers[0]]]
    all_to_all x2 -> x0, starting transfers between devices: 19.2 us -> none  [the longest x1 13.7 us: body(): lax.all_to_all(outgoing, GRAPH, split_axis=0, concat_axis=0, tiled=True)]
    all_to_all x2 -> x0, waiting for transfers between devices: 16.6 us -> none  [the longest x1 16.6 us: from_everyone(): lax.all_to_all(jnp.broadcast_to(shard[None], (count, *shard.shape)), axis...]
    another operation x5 -> x0, other arithmetic: 12.1 us -> none  [the longest x3 6.52 us: body(): factor = jnp.linalg.cholesky(gram)]
    all_to_all x4 -> x0, other arithmetic: 4.74 us -> none  [the longest x3 3.79 us: from_everyone(): lax.all_to_all(jnp.broadcast_to(shard[None], (count, *shard.shape)), axis...]
  transfers between devices with their start and end apart: 2 -> 0, of which waited for: 1 -> 0; matrix products, arithmetic and copies ran while one was open for 7% -> 0% of each run, Pallas kernels for 0% -> 0%
where the time goes in v1:
time: 79.1 us; the launch traced here: 78.8 us
  Pallas kernels  71.8 us (91%)
  local copies, waits for them, and re-layouts  6.38 us (8%)
    pallas_call x1, Pallas kernels, layer(): pl.pallas_call(functools.partial(kernel, sizes), out_shape=(jax.ShapeDtyp...  71.8 us
    unnamed x4, local copies, waits for them, and re-layouts  6.38 us

profile of v1, /device:TPU:1, one launch (start us, length us, event | category | flops | bytes accessed | tf_op | source)
XLA Modules:
  0.0 78.8 jit_solution(820930133322734508)
XLA Ops:
  0.6 71.8 %shard_map.129 = (bf16[512,512]{1,0:T(8,128)(2,1)}, f32[32,512]{1,0:T(8,128)}, f32[32,512]{1,0:T(8,128)}, f32[64,512]{1,0:T(8,128)}) custom-call(bf16[512,512]{1,0:T(8,128)(2,1)} %bitcast.12, bf16[2048,512]{1,0:T(8,128)(2,1)} %bitcast.11, s32[16,128]{1,0:T(8,128)} %bitcast.19, s32[16,128]{1,0:T(8,128)} %bitcast.20, s32[2,128]{1,0:T(2,128)} %bitcast.21, ...), custom_call_target="tpu_custom_call" | custom-call | tf_op jit(solution)/shard_map/pallas_call | solution.py:495
  72.4 1.9 %copy.18 = bf16[1,512,512]{2,1,0:T(8,128)(2,1)} copy(bf16[1,512,512]{2,1,0:T(8,128)(2,1)} %bitcast.14) | data formatting | bytes 1048576
  74.3 1.5 %copy.19 = f32[32,512]{1,0:T(8,128)} copy(f32[32,512]{1,0:T(8,128)} %get-tuple-element.17) | data formatting | bytes 131072
  75.8 1.5 %copy.20 = f32[1,32,512]{2,1,0:T(8,128)} copy(f32[1,32,512]{2,1,0:T(8,128)} %bitcast.18) | data formatting | bytes 131072
  77.3 1.6 %copy.21 = f32[512,64]{0,1:T(8,128)} copy(f32[512,64]{0,1:T(8,128)} %bitcast.16) | data formatting | bytes 262144

commit v2 on v1

--- a/solution.py
+++ b/solution.py
@@ -92,6 +92,7 @@
     pick_halo,
     incidence,
     total,
+    node_top,
     new_block,
     delta,
     inputs_t,
@@ -112,6 +113,9 @@
     x_in,
     q_out,
     q_in,
+    gram_half,
+    gram_out,
+    gram_in,
     halo_s,
     halo_r,
     ax_s,
@@ -130,6 +134,8 @@
     x_r,
     q_s,
     q_r,
+    gram_s,
+    gram_r,
 ):
     nz, nx, ny, nc, cut, tile = sizes
     ng, nd = nz * nx, ny * nc
@@ -218,15 +224,30 @@
 
     pl.semaphore_wait(barrier, ng - 1 + nd - 1)
 
-    def halo_copy(o):
-        to = lax.rem(part + o, ng)
+    z_order = sorted(range(1, nz), key=lambda o: -min(o, nz - o))
+    x_order = sorted(range(1, nx), key=lambda o: -min(o, nx - o))
+    y_order = sorted(range(1, ny), key=lambda o: -min(o, ny - o))
+
+    def z_at(o):
+        return lax.rem(z + o, nz)
+
+    def x_at(o):
+        return lax.rem(x + o, nx)
+
+    def halo_copy(i, oz, ox):
+        to = z_at(oz) * nx + x_at(ox)
         return remote(
-            halo_out.at[to], halo_in.at[part], halo_s.at[o - 1], halo_r.at[o - 1], on_graph(to)
-        )
-
-    @pl.loop(1, ng)
-    def _(o):
-        halo_copy(o).start()
+            halo_out.at[to],
+            halo_in.at[part],
+            halo_s.at[i],
+            halo_r.at[i],
+            (z_at(oz), x_at(ox), y, c),
+        )
+
+    halo_steps = [(oz, ox) for oz in z_order + [0] for ox in x_order + [0] if oz or ox]
+    halo_copies = [halo_copy(i, *step) for i, step in enumerate(halo_steps)]
+    for copy in halo_copies:
+        copy.start()
 
     loads[2].wait()
     loads[3].wait()
@@ -258,9 +279,10 @@
 
     inputs_t[:width, :] = node[...].astype(F32).T.astype(BF)
 
-    @pl.loop(1, ng)
-    def _(o):
-        halo_copy(o).wait()
+    loads[6].wait()
+    node_top[...] = mm(node[...], w_node[:width, :])
+    for copy in halo_copies:
+        copy.wait()
 
     flat = halo_in[...].reshape(ng * 2 * peer, half)
     left_half = mm(flat, w_edge[width : width + half, :]).reshape(ng, 2, peer, width)
@@ -276,10 +298,9 @@
         fresh = (edge[at, :].astype(F32) + value * sigmoid(value)).astype(BF)
         total[...] += mm(incidence[t], fresh)
 
-    loads[6].wait()
     loads[7].wait()
     summed = total[...].astype(BF)
-    node_pre = mm(node[...], w_node[:width, :]) + mm(summed, w_node[width:, :])
+    node_pre = node_top[...] + mm(summed, w_node[width:, :])
     gate = sigmoid(node_pre)
     delta[...] = (cot[...].astype(F32) * (gate * (1.0 + node_pre * (1.0 - gate)))).astype(BF)
     new_block[...] = (node[...].astype(F32) + node_pre * gate).astype(BF)
@@ -288,26 +309,7 @@
     inputs_t[width:, :] = total[...].T.astype(BF)
 
     share = 2 * width // ng
-    step = min(nz, max(1, 256 // (nx * share)))
-
-    @pl.loop(0, nz // step)
-    def _(i):
-        lines = step * nx * share
-        grad = mm(inputs_t[pl.ds(pl.multiple_of(i * lines, lines), lines), :], delta[...])
-        at = pl.ds(i * step, step)
-        grad_a[at] = grad[:, :cut].reshape(step, nx, share, cut).astype(BF)
-        grad_b[at] = grad[:, cut:].reshape(step, nx, share, width - cut).astype(BF)
-
-    z_order = sorted(range(1, nz), key=lambda o: -min(o, nz - o))
-    x_order = sorted(range(1, nx), key=lambda o: -min(o, nx - o))
     turns = z_order + [0]
-
-    def z_at(o):
-        return lax.rem(z + o, nz)
-
-    def x_at(o):
-        return lax.rem(x + o, nx)
-
     bz = {
         o: remote(
             grad_b.at[z_at(o)], bz_in.at[o - 1], bz_s.at[o - 1], bz_r.at[o - 1], on_z(z_at(o))
@@ -335,10 +337,16 @@
         )
         for o in x_order
     }
-    for copy in bz.values():
-        copy.start()
-    for copy in ax.values():
-        copy.start()
+    lines = nx * share
+    for t in turns:
+        at = pl.ds(pl.multiple_of(z_at(t) * lines, lines), lines)
+        grad = mm(inputs_t[at, :], delta[...])
+        grad_a[z_at(t)] = grad[:, :cut].reshape(nx, share, cut).astype(BF)
+        grad_b[z_at(t)] = grad[:, cut:].reshape(nx, share, width - cut).astype(BF)
+        for o in x_order:
+            ax[t, o].start()
+        if t:
+            bz[t].start()
     for t in turns:
         value = grad_a[z_at(t), x].astype(F32)
         for o in x_order:
@@ -381,17 +389,24 @@
     dp_out[:, piece:, :] = jnp.broadcast_to(packed[None], (nd, *packed.shape))
     dp_in[pl.ds(group, 1)] = dp_out[pl.ds(group, 1)]
 
-    def dp_copy(o):
-        to = lax.rem(group + o, nd)
-        return remote(dp_out.at[to], dp_in.at[group], dp_s.at[o - 1], dp_r.at[o - 1], on_dp(to))
-
-    @pl.loop(1, nd)
-    def _(o):
-        dp_copy(o).start()
-
-    @pl.loop(1, nd)
-    def _(o):
-        dp_copy(o).wait()
+    dp_steps = [(oy, oc) for oy in y_order + [0] for oc in range(nc) if oy or oc]
+
+    def dp_at(oy, oc):
+        return (z, x, lax.rem(y + oy, ny), lax.rem(c + oc, nc))
+
+    def member(device):
+        return device[2] * nc + device[3]
+
+    dp_copies = []
+    for i, step in enumerate(dp_steps):
+        to = dp_at(*step)
+        dp_copies.append(
+            remote(dp_out.at[member(to)], dp_in.at[group], dp_s.at[i], dp_r.at[i], to)
+        )
+    for copy in dp_copies:
+        copy.start()
+    for copy in dp_copies:
+        copy.wait()
 
     arrived = jnp.sum(dp_in[...], axis=0)
     columns, packed = arrived[:piece], arrived[piece:]
@@ -405,7 +420,9 @@
     for h in range(halves):
         chosen = jnp.where(owner == pack * h + side, spread, 0.0)
         z_out[h * piece : (h + 1) * piece, :] = mm(columns, chosen, precision=HIGH)
-    z_out[halves * piece :, :] = jnp.concatenate([gram[: rank // 2], gram[rank // 2 :]], axis=1)
+    both_parts = jnp.concatenate([gram[: rank // 2], gram[rank // 2 :]], axis=1)
+    gram_half[...] = both_parts.reshape(nc, rank // 2 // nc, LANE)
+    z_out[halves * piece :, :] = gram_half[c]
 
     z_in[pl.ds(z, 1)] = z_out[...][None]
     zs = {
@@ -431,22 +448,26 @@
     q_out[...] = both[: halves * piece]
     q_in[pl.ds(group, 1)] = q_out[...][None]
 
-    def q_copy(o):
-        to = lax.rem(group + o, nd)
-        return remote(q_out, q_in.at[group], q_s.at[o - 1], q_r.at[o - 1], on_dp(to))
-
-    @pl.loop(1, nd)
-    def _(o):
-        q_copy(o).start()
-
-    packed = both[halves * piece :]
+    q_copies = [
+        remote(q_out, q_in.at[group], q_s.at[i], q_r.at[i], dp_at(*step))
+        for i, step in enumerate(dp_steps)
+    ]
+    swap = remote(
+        gram_out, gram_in.at[c], gram_s.at[0], gram_r.at[0], (z, x, y, lax.rem(c + 1, nc))
+    )
+    gram_out[...] = both[halves * piece :]
+    gram_in[pl.ds(c, 1)] = gram_out[...][None]
+    swap.start()
+    for copy in q_copies:
+        copy.start()
+    swap.wait()
+    packed = gram_in[...].reshape(rank // 2, LANE)
     gram = jnp.concatenate([packed[:, :rank], packed[:, rank:]], axis=0)
     inverse = inverse_factor(gram)
     ortho = mm(left, inverse, ((1,), (1,)), HIGH)
 
-    @pl.loop(1, nd)
-    def _(o):
-        q_copy(o).wait()
+    for copy in q_copies:
+        copy.wait()
 
     for h in range(halves):
         right = q_in[:, h * piece : (h + 1) * piece, :].reshape(LANE, LANE)
@@ -463,6 +484,30 @@
         for copy in copies.values():
             copy.wait_send()
     store.wait()
+
+
+def put(count, *refs):
+    sources, results, sem = refs[:count], refs[count:-1], refs[-1]
+    copies = [
+        pltpu.make_async_copy(source, result, sem.at[i])
+        for i, (source, result) in enumerate(zip(sources, results))
+    ]
+    for copy in copies:
+        copy.start()
+    for copy in copies:
+        copy.wait()
+
+
+def settled(*arrays):
+    count = len(arrays)
+    return pl.pallas_call(
+        functools.partial(put, count),
+        out_shape=tuple(jax.ShapeDtypeStruct(a.shape, a.dtype) for a in arrays),
+        in_specs=[pl.BlockSpec(memory_space=pltpu.VMEM)] * count,
+        out_specs=tuple([pl.BlockSpec(memory_space=pltpu.MemorySpace.HBM)] * count),
+        scratch_shapes=[pltpu.SemaphoreType.DMA((count,))],
+        compiler_params=pltpu.CompilerParams(vmem_limit_bytes=67043328),
+    )(*arrays)
 
 
 def layer(
@@ -491,7 +536,7 @@
     hbm = pl.BlockSpec(memory_space=pltpu.MemorySpace.HBM)
     vmem = pl.BlockSpec(memory_space=pltpu.VMEM)
     dma = pltpu.SemaphoreType.DMA
-    exchange = halves * piece + rank // 2
+    exchange = halves * piece + rank // 2 // nc
     new_block, update, new_error, new_q = pl.pallas_call(
         functools.partial(kernel, sizes),
         out_shape=(
@@ -524,6 +569,7 @@
             pltpu.VMEM((edges, halo), BF),
             pltpu.VMEM((edges // tile, count, tile), BF),
             pltpu.VMEM((count, width), F32),
+            pltpu.VMEM((count, width), F32),
             pltpu.VMEM((count, width), BF),
             pltpu.VMEM((count, width), BF),
             pltpu.VMEM((2 * width, count), BF),
@@ -544,6 +590,9 @@
             pltpu.VMEM((nx, exchange, LANE), F32),
             pltpu.VMEM((halves * piece, LANE), F32),
             pltpu.VMEM((nd, halves * piece, LANE), F32),
+            pltpu.VMEM((nc, rank // 2 // nc, LANE), F32),
+            pltpu.VMEM((rank // 2 // nc, LANE), F32),
+            pltpu.VMEM((nc, rank // 2 // nc, LANE), F32),
             dma((ng - 1,)),
             dma((ng - 1,)),
             dma((nx - 1, nz)),
@@ -562,6 +611,8 @@
             dma((nx - 1,)),
             dma((nd - 1,)),
             dma((nd - 1,)),
+            dma((1,)),
+            dma((1,)),
         ],
         compiler_params=pltpu.CompilerParams(
             collective_id=0, has_side_effects=True, vmem_limit_bytes=67043328
@@ -578,6 +629,7 @@
         error_memory[0],
         warm_q.T,
     )
+    new_block, update, new_error, new_q = settled(new_block, update, new_error, new_q)
     return new_block[None], update, new_error[None], new_q.T
 
 

time: 79.1 us -> 73.7 us (0.932)
  local copies, waits for them, and re-layouts: 6.38 us -> 0 us
  Pallas kernels: 71.8 us -> 72.9 us
    unnamed x4 -> x0, local copies, waits for them, and re-layouts: 6.38 us -> none
    pallas_call x0 -> x1, Pallas kernels: none -> 2.03 us  [settled(): pl.pallas_call(functools.partial(put, count), out_shape=tuple((jax.ShapeD...]
    pallas_call x1, Pallas kernels: 71.8 us -> 70.9 us  [layer(): pl.pallas_call(functools.partial(kernel, sizes), out_shape=(jax.ShapeDtyp...]
where the time goes in v2:
time: 73.7 us; the launch traced here: 73.5 us
  Pallas kernels  72.9 us (99%)
    pallas_call x1, Pallas kernels, layer(): pl.pallas_call(functools.partial(kernel, sizes), out_shape=(jax.ShapeDtyp...  70.9 us
    pallas_call x1, Pallas kernels, settled(): pl.pallas_call(functools.partial(put, count), out_shape=tuple((jax.ShapeD...  2.03 us

profile of v2, /device:TPU:1, one launch (start us, length us, event | category | flops | bytes accessed | tf_op | source)
XLA Modules:
  0.0 73.5 jit_solution(11190413612401409181)
XLA Ops:
  0.6 70.9 %shard_map.129 = (bf16[512,512]{1,0:T(8,128)(2,1)}, f32[32,512]{1,0:T(8,128)}, f32[32,512]{1,0:T(8,128)}, f32[64,512]{1,0:T(8,128)}) custom-call(bf16[512,512]{1,0:T(8,128)(2,1)} %bitcast.12, bf16[2048,512]{1,0:T(8,128)(2,1)} %bitcast.11, s32[16,128]{1,0:T(8,128)} %bitcast.16, s32[16,128]{1,0:T(8,128)} %bitcast.17, s32[2,128]{1,0:T(2,128)} %bitcast.18, ...), custom_call_target="tpu_custom_call" | custom-call | tf_op jit(solution)/shard_map/pallas_call | solution.py:540
  71.5 2.0 %shard_map.130 = (bf16[512,512]{1,0:T(8,128)(2,1)}, f32[32,512]{1,0:T(8,128)}, f32[32,512]{1,0:T(8,128)}, f32[64,512]{1,0:T(8,128)}) custom-call(bf16[512,512]{1,0:T(8,128)(2,1)} %get-tuple-element.12.refs_0_, f32[32,512]{1,0:T(8,128)} %get-tuple-element.13.refs_1_, f32[32,512]{1,0:T(8,128)} %get-tuple-element.14.refs_2_, f32[64,512]{1,0:T(8,128)} %get-tuple-element.15.refs_3_), custom_call_target="tpu_custom_call" | custom-call | tf_op jit(solution)/shard_map/pallas_call | solution.py:503

commit v3 on v2

--- a/solution.py
+++ b/solution.py
@@ -114,6 +114,10 @@
     q_out,
     q_in,
     gram_half,
+    zg_out,
+    zg_in,
+    xg_out,
+    xg_in,
     gram_out,
     gram_in,
     halo_s,
@@ -136,6 +140,10 @@
     q_r,
     gram_s,
     gram_r,
+    zg_s,
+    zg_r,
+    xg_s,
+    xg_r,
 ):
     nz, nx, ny, nc, cut, tile = sizes
     ng, nd = nz * nx, ny * nc
@@ -227,6 +235,7 @@
     z_order = sorted(range(1, nz), key=lambda o: -min(o, nz - o))
     x_order = sorted(range(1, nx), key=lambda o: -min(o, nx - o))
     y_order = sorted(range(1, ny), key=lambda o: -min(o, ny - o))
+    z_near = sorted(range(1, nz), key=lambda o: min(o, nz - o))
 
     def z_at(o):
         return lax.rem(z + o, nz)
@@ -244,7 +253,7 @@
             (z_at(oz), x_at(ox), y, c),
         )
 
-    halo_steps = [(oz, ox) for oz in z_order + [0] for ox in x_order + [0] if oz or ox]
+    halo_steps = [(oz, ox) for ox in range(nx) for oz in z_near + [0] if oz or ox]
     halo_copies = [halo_copy(i, *step) for i, step in enumerate(halo_steps)]
     for copy in halo_copies:
         copy.start()
@@ -422,42 +431,56 @@
         z_out[h * piece : (h + 1) * piece, :] = mm(columns, chosen, precision=HIGH)
     both_parts = jnp.concatenate([gram[: rank // 2], gram[rank // 2 :]], axis=1)
     gram_half[...] = both_parts.reshape(nc, rank // 2 // nc, LANE)
-    z_out[halves * piece :, :] = gram_half[c]
-
-    z_in[pl.ds(z, 1)] = z_out[...][None]
-    zs = {
-        o: remote(z_out, z_in.at[z], z_s.at[o - 1], z_r.at[o - 1], on_z(z_at(o)))
-        for o in z_order
-    }
-    for copy in zs.values():
-        copy.start()
-    for copy in zs.values():
+    zg_out[...] = gram_half[c]
+
+    def to_all(order, out, into, me, send, recv, device):
+        into[pl.ds(me, 1)] = out[...][None]
+        return [
+            remote(out, into.at[me], send.at[o - 1], recv.at[o - 1], device(o)) for o in order
+        ]
+
+    def along_z(o):
+        return on_z(z_at(o))
+
+    def along_x(o):
+        return on_x(x_at(o))
+
+    zg = to_all(z_order, zg_out, zg_in, z, zg_s, zg_r, along_z)
+    for copy in zg:
+        copy.start()
+    zs = to_all(z_order, z_out, z_in, z, z_s, z_r, along_z)
+    for copy in zs:
+        copy.start()
+    for copy in zg:
+        copy.wait()
+    xg_out[...] = jnp.sum(zg_in[...], axis=0)
+    xg = to_all(x_order, xg_out, xg_in, x, xg_s, xg_r, along_x)
+    for copy in xg:
+        copy.start()
+    for copy in zs:
         copy.wait()
     x_out[...] = jnp.sum(z_in[...], axis=0)
-    x_in[pl.ds(x, 1)] = x_out[...][None]
-    xs = {
-        o: remote(x_out, x_in.at[x], x_s.at[o - 1], x_r.at[o - 1], on_x(x_at(o)))
-        for o in x_order
-    }
-    for copy in xs.values():
-        copy.start()
-    for copy in xs.values():
-        copy.wait()
-    both = jnp.sum(x_in[...], axis=0)
-
-    q_out[...] = both[: halves * piece]
+    xs = to_all(x_order, x_out, x_in, x, x_s, x_r, along_x)
+    for copy in xs:
+        copy.start()
+    for copy in xg:
+        copy.wait()
+    gram_out[...] = jnp.sum(xg_in[...], axis=0)
+    gram_in[pl.ds(c, 1)] = gram_out[...][None]
+    swap = remote(
+        gram_out, gram_in.at[c], gram_s.at[0], gram_r.at[0], (z, x, y, lax.rem(c + 1, nc))
+    )
+    swap.start()
+    for copy in xs:
+        copy.wait()
+
+    q_out[...] = jnp.sum(x_in[...], axis=0)
     q_in[pl.ds(group, 1)] = q_out[...][None]
 
     q_copies = [
         remote(q_out, q_in.at[group], q_s.at[i], q_r.at[i], dp_at(*step))
         for i, step in enumerate(dp_steps)
     ]
-    swap = remote(
-        gram_out, gram_in.at[c], gram_s.at[0], gram_r.at[0], (z, x, y, lax.rem(c + 1, nc))
-    )
-    gram_out[...] = both[halves * piece :]
-    gram_in[pl.ds(c, 1)] = gram_out[...][None]
-    swap.start()
     for copy in q_copies:
         copy.start()
     swap.wait()
@@ -536,7 +559,8 @@
     hbm = pl.BlockSpec(memory_space=pltpu.MemorySpace.HBM)
     vmem = pl.BlockSpec(memory_space=pltpu.VMEM)
     dma = pltpu.SemaphoreType.DMA
-    exchange = halves * piece + rank // 2 // nc
+    exchange = halves * piece
+    gram_rows = rank // 2 // nc
     new_block, update, new_error, new_q = pl.pallas_call(
         functools.partial(kernel, sizes),
         out_shape=(
@@ -590,9 +614,13 @@
             pltpu.VMEM((nx, exchange, LANE), F32),
             pltpu.VMEM((halves * piece, LANE), F32),
             pltpu.VMEM((nd, halves * piece, LANE), F32),
-            pltpu.VMEM((nc, rank // 2 // nc, LANE), F32),
-            pltpu.VMEM((rank // 2 // nc, LANE), F32),
-            pltpu.VMEM((nc, rank // 2 // nc, LANE), F32),
+            pltpu.VMEM((nc, gram_rows, LANE), F32),
+            pltpu.VMEM((gram_rows, LANE), F32),
+            pltpu.VMEM((nz, gram_rows, LANE), F32),
+            pltpu.VMEM((gram_rows, LANE), F32),
+            pltpu.VMEM((nx, gram_rows, LANE), F32),
+            pltpu.VMEM((gram_rows, LANE), F32),
+            pltpu.VMEM((nc, gram_rows, LANE), F32),
             dma((ng - 1,)),
             dma((ng - 1,)),
             dma((nx - 1, nz)),
@@ -613,6 +641,10 @@
             dma((nd - 1,)),
             dma((1,)),
             dma((1,)),
+            dma((nz - 1,)),
+            dma((nz - 1,)),
+            dma((nx - 1,)),
+            dma((nx - 1,)),
         ],
         compiler_params=pltpu.CompilerParams(
             collective_id=0, has_side_effects=True, vmem_limit_bytes=67043328

time: 73.7 us -> 73.1 us (level)
  no operation moved by 1% of the time
where the time goes in v3:
time: 73.1 us; the launch traced here: 73 us
  Pallas kernels  72.3 us (99%)
    pallas_call x1, Pallas kernels, layer(): pl.pallas_call(functools.partial(kernel, sizes), out_shape=(jax.ShapeDtyp...  70.3 us
    pallas_call x1, Pallas kernels, settled(): pl.pallas_call(functools.partial(put, count), out_shape=tuple((jax.ShapeD...  2.03 us

profile of v3, /device:TPU:1, one launch (start us, length us, event | category | flops | bytes accessed | tf_op | source)
XLA Modules:
  0.0 73.0 jit_solution(9049320638501219889)
XLA Ops:
  0.6 70.3 %shard_map.129 = (bf16[512,512]{1,0:T(8,128)(2,1)}, f32[32,512]{1,0:T(8,128)}, f32[32,512]{1,0:T(8,128)}, f32[64,512]{1,0:T(8,128)}) custom-call(bf16[512,512]{1,0:T(8,128)(2,1)} %bitcast.12, bf16[2048,512]{1,0:T(8,128)(2,1)} %bitcast.11, s32[16,128]{1,0:T(8,128)} %bitcast.16, s32[16,128]{1,0:T(8,128)} %bitcast.17, s32[2,128]{1,0:T(2,128)} %bitcast.18, ...), custom_call_target="tpu_custom_call" | custom-call | tf_op jit(solution)/shard_map/pallas_call | solution.py:564
  71.0 2.0 %shard_map.130 = (bf16[512,512]{1,0:T(8,128)(2,1)}, f32[32,512]{1,0:T(8,128)}, f32[32,512]{1,0:T(8,128)}, f32[64,512]{1,0:T(8,128)}) custom-call(bf16[512,512]{1,0:T(8,128)(2,1)} %get-tuple-element.12.refs_0_, f32[32,512]{1,0:T(8,128)} %get-tuple-element.13.refs_1_, f32[32,512]{1,0:T(8,128)} %get-tuple-element.14.refs_2_, f32[64,512]{1,0:T(8,128)} %get-tuple-element.15.refs_3_), custom_call_target="tpu_custom_call" | custom-call | tf_op jit(solution)/shard_map/pallas_call | solution.py:526
